TPU v7x, 32 devices: a 4x4x1 block of a 4x4x8 slice. The times are simulated.
32 devices in a mesh: batch: 1 (over z), seq_hi: 4 (over y), seq: 8 (over x, core).
Axes of the slice: x: 4, y: 4, z: 1, core: 2. Of those that a mesh axis runs over, the one named last changes fastest.
The devices are a block of a 4x4x8 slice.
Arguments:
- x_seq: bfloat16 [32, 1024, 512], P('batch', ('seq_hi', 'seq'))
- w_f0: bfloat16 [3, 10, 512, 512], replicated
- w_f1: bfloat16 [3, 10, 512, 512], replicated
- w_g0: bfloat16 [3, 10, 512, 512], replicated
- w_g1: bfloat16 [3, 10, 512, 512], replicated
- w_res: bfloat16 [3, 10, 512, 512], replicated
- w_skip: bfloat16 [3, 10, 512, 256], replicated
Outputs:
- output 1: float32 [32, 1024, 512], P('batch', ('seq_hi', 'seq'))
- output 2: float32 [32, 1024, 256], P('batch', ('seq_hi', 'seq'))
All inputs are finite; a program needn't handle non-finite values.
Results may differ from a plain program's by a relative error of at most 0.00955824.
Values are sent between devices in bfloat16 or wider.
A program may use at most 768 MiB of HBM per device.

v0:
```python
import jax
import jax.numpy as jnp
from jax import lax
from jax.sharding import PartitionSpec as P

SEQ_AXES = ("seq_hi", "seq")


def move_right(block, hops, n_shards):
    if hops >= n_shards:
        return jnp.zeros_like(block)
    return lax.ppermute(block, SEQ_AXES, perm=[(source, source + hops) for source in range(n_shards - hops)])


def delay_rows(current, dilation, n_shards):
    local_len = current.shape[1]
    hops, rest = divmod(dilation, local_len)
    pieces = []
    if rest > 0:
        pieces.append(move_right(current[:, local_len - rest:], hops + 1, n_shards))
    if hops > 0:
        pieces.append(move_right(current[:, :local_len - rest], hops, n_shards))
    else:
        pieces.append(current[:, :local_len - rest])
    if len(pieces) == 1:
        return pieces[0]
    return jnp.concatenate(pieces, axis=1)


def gated_layer(residual, skip_acc, current, delayed, w_cur, w_del, w_out):
    chans = residual.shape[-1]
    gates = jnp.einsum("bsc,cd->bsd", current, w_cur, preferred_element_type=jnp.float32) + jnp.einsum("bsc,cd->bsd", delayed, w_del, preferred_element_type=jnp.float32)
    activated = (jnp.tanh(gates[..., :chans]) * jax.nn.sigmoid(gates[..., chans:])).astype(jnp.bfloat16)
    mixed = jnp.einsum("bsc,cd->bsd", activated, w_out, preferred_element_type=jnp.float32)
    return residual + mixed[..., :chans], skip_acc + mixed[..., chans:]


def solution(mesh):
    n_shards = mesh.shape["seq_hi"] * mesh.shape["seq"]
    seq_spec = P("batch", SEQ_AXES, None)

    def local_stack(x_loc, w_f0, w_f1, w_g0, w_g1, w_res, w_skip):
        n_rep, n_cyc = w_f0.shape[0], w_f0.shape[1]
        w_cur = jnp.concatenate([w_f1, w_g1], axis=-1)
        w_del = jnp.concatenate([w_f0, w_g0], axis=-1)
        w_out = jnp.concatenate([w_res, w_skip], axis=-1)
        residual = x_loc.astype(jnp.float32)
        skip_acc = jnp.zeros(x_loc.shape[:2] + (w_skip.shape[-1],), jnp.float32)
        for rep_idx in range(n_rep):
            for cyc_idx in range(n_cyc):
                current = residual.astype(jnp.bfloat16)
                delayed = delay_rows(current, 2 ** cyc_idx, n_shards)
                residual, skip_acc = gated_layer(residual, skip_acc, current, delayed, w_cur[rep_idx, cyc_idx], w_del[rep_idx, cyc_idx], w_out[rep_idx, cyc_idx])
        return residual, skip_acc

    return jax.shard_map(local_stack, mesh=mesh, in_specs=(seq_spec, P(), P(), P(), P(), P(), P()), out_specs=(seq_spec, seq_spec), check_vma=False)
```

profile of v0, /device:TPU:120, one launch (start us, length us, event | category | flops | bytes accessed | tf_op | source)
XLA Modules:
  0.0 848.5 jit_solution(12597979073651008778)
XLA Ops:
  3.6 14.2 %constant_dynamic-update-slice_fusion.5 = bf16[3,10,512,768]{3,2,1,0:T(8,128)(2,1)} fusion(bf16[3,10,512,512]{3,2,1,0:T(8,128)(2,1)} %param.12), kind=kLoop, calls=%fused_computation.514 | loop fusion | bytes 31457280
  26.3 8.4 constant_dynamic-update-slice_fusion.1
  34.7 8.7 %constant_dynamic-update-slice_fusion = bf16[3,10,512,1024]{3,2,1,0:T(8,128)(2,1)S(1)} fusion(bf16[3,10,512,1024]{3,2,1,0:T(8,128)(2,1)S(1)} %constant_dynamic-update-slice_fusion.1, bf16[3,10,512,512]{3,2,1,0:T(8,128)(2,1)} %param.11), kind=kLoop, calls=%fused_computation.509 | loop fusion | bytes 31457280 | tf_op jit(solution)/shard_map/concatenate | solution.py:44
  43.5 10.4 %copy-done = bf16[3,10,512,1024]{3,2,1,0:T(8,128)(2,1)} copy-done((bf16[3,10,512,1024]{3,2,1,0:T(8,128)(2,1)}, bf16[3,10,512,1024]{3,2,1,0:T(8,128)(2,1)S(1)}, u32[]{:S(2)}) %copy-start) | copy-done | bytes 31457304
  55.1 13.4 %constant_dynamic-update-slice_fusion.2 = bf16[3,10,512,1024]{3,2,1,0:T(8,128)(2,1)} fusion(bf16[3,10,512,1024]{3,2,1,0:T(8,128)(2,1)} %constant_dynamic-update-slice_fusion.3, bf16[3,10,512,512]{3,2,1,0:T(8,128)(2,1)} %param.10), kind=kLoop, calls=%fused_computation.511 | loop fusion | bytes 31457280 | tf_op jit(solution)/shard_map/concatenate | solution.py:45
  145.7 9.0 %collective-permute-done.4 = bf16[32,16,512]{2,1,0:T(8,128)(2,1)S(1)} collective-permute-done((bf16[32,16,512]{2,1,0:T(8,128)(2,1)S(1)}, bf16[32,16,512]{2,1,0:T(8,128)(2,1)S(1)}, u32[]{:S(2)}, u32[]{:S(2)}) %collective-permute-start.4) | collective-permute-done | bytes 524320 | tf_op jit(solution)/shard_map/ppermute | solution.py:12
  164.7 15.0 %collective-permute-done.5 = bf16[32,32,512]{2,1,0:T(8,128)(2,1)S(1)} collective-permute-done((bf16[32,32,512]{2,1,0:T(8,128)(2,1)S(1)}, bf16[32,32,512]{2,1,0:T(8,128)(2,1)S(1)}, u32[]{:S(2)}, u32[]{:S(2)}) %collective-permute-start.5) | collective-permute-done | bytes 1048608 | tf_op jit(solution)/shard_map/ppermute | solution.py:12
  193.0 22.0 %collective-permute-done.6 = bf16[32,32,512]{2,1,0:T(8,128)(2,1)S(1)} collective-permute-done((bf16[32,32,512]{2,1,0:T(8,128)(2,1)S(1)}, bf16[32,32,512]{2,1,0:T(8,128)(2,1)S(1)}, u32[]{:S(2)}, u32[]{:S(2)}) %collective-permute-start.6) | collective-permute-done | bytes 1048608 | tf_op jit(solution)/shard_map/ppermute | solution.py:12
  228.3 21.3 %collective-permute-done.7 = bf16[32,32,512]{2,1,0:T(8,128)(2,1)S(1)} collective-permute-done((bf16[32,32,512]{2,1,0:T(8,128)(2,1)S(1)}, bf16[32,32,512]{2,1,0:T(8,128)(2,1)S(1)}, u32[]{:S(2)}, u32[]{:S(2)}) %collective-permute-start.7) | collective-permute-done | bytes 1048608 | tf_op jit(solution)/shard_map/ppermute | solution.py:12
  265.6 17.6 %collective-permute-done.8 = bf16[32,32,512]{2,1,0:T(8,128)(2,1)S(1)} collective-permute-done((bf16[32,32,512]{2,1,0:T(8,128)(2,1)S(1)}, bf16[32,32,512]{2,1,0:T(8,128)(2,1)S(1)}, u32[]{:S(2)}, u32[]{:S(2)}) %collective-permute-start.8) | collective-permute-done | bytes 1048608 | tf_op jit(solution)/shard_map/ppermute | solution.py:12
  292.7 18.4 %collective-permute-done.9 = bf16[32,32,512]{2,1,0:T(8,128)(2,1)S(1)} collective-permute-done((bf16[32,32,512]{2,1,0:T(8,128)(2,1)S(1)}, bf16[32,32,512]{2,1,0:T(8,128)(2,1)S(1)}, u32[]{:S(2)}, u32[]{:S(2)}) %collective-permute-start.9) | collective-permute-done | bytes 1048608 | tf_op jit(solution)/shard_map/ppermute | solution.py:12
  402.4 9.4 %collective-permute-done.14 = bf16[32,16,512]{2,1,0:T(8,128)(2,1)S(1)} collective-permute-done((bf16[32,16,512]{2,1,0:T(8,128)(2,1)S(1)}, bf16[32,16,512]{2,1,0:T(8,128)(2,1)S(1)}, u32[]{:S(2)}, u32[]{:S(2)}) %collective-permute-start.14) | collective-permute-done | bytes 524320 | tf_op jit(solution)/shard_map/ppermute | solution.py:12
  425.2 14.9 %collective-permute-done.15 = bf16[32,32,512]{2,1,0:T(8,128)(2,1)S(1)} collective-permute-done((bf16[32,32,512]{2,1,0:T(8,128)(2,1)S(1)}, bf16[32,32,512]{2,1,0:T(8,128)(2,1)S(1)}, u32[]{:S(2)}, u32[]{:S(2)}) %collective-permute-start.15) | collective-permute-done | bytes 1048608 | tf_op jit(solution)/shard_map/ppermute | solution.py:12
  456.5 22.0 %collective-permute-done.16 = bf16[32,32,512]{2,1,0:T(8,128)(2,1)S(1)} collective-permute-done((bf16[32,32,512]{2,1,0:T(8,128)(2,1)S(1)}, bf16[32,32,512]{2,1,0:T(8,128)(2,1)S(1)}, u32[]{:S(2)}, u32[]{:S(2)}) %collective-permute-start.16) | collective-permute-done | bytes 1048608 | tf_op jit(solution)/shard_map/ppermute | solution.py:12
  488.6 21.2 %collective-permute-done.17 = bf16[32,32,512]{2,1,0:T(8,128)(2,1)S(1)} collective-permute-done((bf16[32,32,512]{2,1,0:T(8,128)(2,1)S(1)}, bf16[32,32,512]{2,1,0:T(8,128)(2,1)S(1)}, u32[]{:S(2)}, u32[]{:S(2)}) %collective-permute-start.17) | collective-permute-done | bytes 1048608 | tf_op jit(solution)/shard_map/ppermute | solution.py:12
  524.6 16.4 %collective-permute-done.18 = bf16[32,32,512]{2,1,0:T(8,128)(2,1)S(1)} collective-permute-done((bf16[32,32,512]{2,1,0:T(8,128)(2,1)}, bf16[32,32,512]{2,1,0:T(8,128)(2,1)S(1)}, u32[]{:S(2)}, u32[]{:S(2)}) %collective-permute-start.18) | collective-permute-done | bytes 1048608 | tf_op jit(solution)/shard_map/ppermute | solution.py:12
  550.5 18.3 %collective-permute-done.19 = bf16[32,32,512]{2,1,0:T(8,128)(2,1)S(1)} collective-permute-done((bf16[32,32,512]{2,1,0:T(8,128)(2,1)S(1)}, bf16[32,32,512]{2,1,0:T(8,128)(2,1)S(1)}, u32[]{:S(2)}, u32[]{:S(2)}) %collective-permute-start.19) | collective-permute-done | bytes 1048608 | tf_op jit(solution)/shard_map/ppermute | solution.py:12
  659.8 9.4 %collective-permute-done.24 = bf16[32,16,512]{2,1,0:T(8,128)(2,1)S(1)} collective-permute-done((bf16[32,16,512]{2,1,0:T(8,128)(2,1)S(1)}, bf16[32,16,512]{2,1,0:T(8,128)(2,1)S(1)}, u32[]{:S(2)}, u32[]{:S(2)}) %collective-permute-start.24) | collective-permute-done | bytes 524320 | tf_op jit(solution)/shard_map/ppermute | solution.py:12
  682.7 14.8 %collective-permute-done.25 = bf16[32,32,512]{2,1,0:T(8,128)(2,1)S(1)} collective-permute-done((bf16[32,32,512]{2,1,0:T(8,128)(2,1)S(1)}, bf16[32,32,512]{2,1,0:T(8,128)(2,1)S(1)}, u32[]{:S(2)}, u32[]{:S(2)}) %collective-permute-start.25) | collective-permute-done | bytes 1048608 | tf_op jit(solution)/shard_map/ppermute | solution.py:12
  716.0 20.7 %collective-permute-done.26 = bf16[32,32,512]{2,1,0:T(8,128)(2,1)S(1)} collective-permute-done((bf16[32,32,512]{2,1,0:T(8,128)(2,1)}, bf16[32,32,512]{2,1,0:T(8,128)(2,1)S(1)}, u32[]{:S(2)}, u32[]{:S(2)}) %collective-permute-start.26) | collective-permute-done | bytes 1048608 | tf_op jit(solution)/shard_map/ppermute | solution.py:12
  747.1 21.2 %collective-permute-done.27 = bf16[32,32,512]{2,1,0:T(8,128)(2,1)S(1)} collective-permute-done((bf16[32,32,512]{2,1,0:T(8,128)(2,1)S(1)}, bf16[32,32,512]{2,1,0:T(8,128)(2,1)S(1)}, u32[]{:S(2)}, u32[]{:S(2)}) %collective-permute-start.27) | collective-permute-done | bytes 1048608 | tf_op jit(solution)/shard_map/ppermute | solution.py:12
  780.8 17.6 %collective-permute-done.28 = bf16[32,32,512]{2,1,0:T(8,128)(2,1)S(1)} collective-permute-done((bf16[32,32,512]{2,1,0:T(8,128)(2,1)S(1)}, bf16[32,32,512]{2,1,0:T(8,128)(2,1)S(1)}, u32[]{:S(2)}, u32[]{:S(2)}) %collective-permute-start.28) | collective-permute-done | bytes 1048608 | tf_op jit(solution)/shard_map/ppermute | solution.py:12
  810.2 18.3 %collective-permute-done.29 = bf16[32,32,512]{2,1,0:T(8,128)(2,1)S(1)} collective-permute-done((bf16[32,32,512]{2,1,0:T(8,128)(2,1)S(1)}, bf16[32,32,512]{2,1,0:T(8,128)(2,1)S(1)}, u32[]{:S(2)}, u32[]{:S(2)}) %collective-permute-start.29) | collective-permute-done | bytes 1048608 | tf_op jit(solution)/shard_map/ppermute | solution.py:12
  833.6 12.4 %slice_add_fusion.30 = f32[32,32,256]{2,1,0:T(8,128)} fusion(f32[32,32,768]{2,1,0:T(8,128)S(1)} %fusion.226, f32[32,32,768]{2,1,0:T(8,128)S(1)} %fusion.228, f32[32,32,768]{2,1,0:T(8,128)} %fusion.230, f32[32,32,768]{2,1,0:T(8,128)} %copy-done.16, f32[32,32,768]{2,1,0:T(8,128)} %fusion.234, f32[32,32,768]{2,1,0:T(8,128)} %copy-done.15, ...), kind=kLoop, calls=%fused_computation.271 | loop fusion | flops 7602176 | bytes 32505856 | tf_op jit(solution)/shard_map/add | solution.py:35
  (232 shorter events, 471.0 us)
Async XLA Ops:
  1.7 74.3 %collective-permute-start = (bf16[32,1,512]{2,1,0:T(2,128)(2,1)S(1)}, bf16[32,1,512]{2,1,0:T(2,128)(2,1)S(1)}, u32[]{:S(2)}, u32[]{:S(2)}) collective-permute-start(bf16[32,1,512]{2,1,0:T(2,128)(2,1)S(1)} %slice.721), channel_id=1, source_target_pairs={{0,1},{1,2},{2,3},{3,4},{4,5},{5,6},{6,7},{7,8},{8,9},{9,10},{10,1... | collective-permute-start | bytes 98312 | tf_op jit(solution)/shard_map/ppermute | solution.py:12
  100.3 8.4 collective-permute-start.2
  118.8 9.8 %collective-permute-start.3 = (bf16[32,8,512]{2,1,0:T(8,128)(2,1)S(1)}, bf16[32,8,512]{2,1,0:T(8,128)(2,1)S(1)}, u32[]{:S(2)}, u32[]{:S(2)}) collective-permute-start(bf16[32,8,512]{2,1,0:T(8,128)(2,1)S(1)} %slice.983), channel_id=1, source_target_pairs={{0,1},{1,2},{2,3},{3,4},{4,5},{5,6},{6,7},{7,8},{8,9},{9,10},{10,1... | collective-permute-start | bytes 786440 | tf_op jit(solution)/shard_map/ppermute | solution.py:12
  142.1 12.6 %collective-permute-start.4 = (bf16[32,16,512]{2,1,0:T(8,128)(2,1)S(1)}, bf16[32,16,512]{2,1,0:T(8,128)(2,1)S(1)}, u32[]{:S(2)}, u32[]{:S(2)}) collective-permute-start(bf16[32,16,512]{2,1,0:T(8,128)(2,1)S(1)} %get-tuple-element.34), channel_id=1, source_target_pairs={{0,1},{1,2},{2,3},{3,4},{4,5},{5,6},{6,7},{7,8},{8,9},{9,10},{10,1... | collective-permute-start | bytes 1572872 | tf_op jit(solution)/shard_map/ppermute | solution.py:12
  161.5 18.2 %collective-permute-start.5 = (bf16[32,32,512]{2,1,0:T(8,128)(2,1)S(1)}, bf16[32,32,512]{2,1,0:T(8,128)(2,1)S(1)}, u32[]{:S(2)}, u32[]{:S(2)}) collective-permute-start(bf16[32,32,512]{2,1,0:T(8,128)(2,1)S(1)} %fusion.287), channel_id=1, source_target_pairs={{0,1},{1,2},{2,3},{3,4},{4,5},{5,6},{6,7},{7,8},{8,9},{9,10},{10,1... | collective-permute-start | bytes 3145736 | tf_op jit(solution)/shard_map/ppermute | solution.py:12
  189.8 25.2 %collective-permute-start.6 = (bf16[32,32,512]{2,1,0:T(8,128)(2,1)S(1)}, bf16[32,32,512]{2,1,0:T(8,128)(2,1)S(1)}, u32[]{:S(2)}, u32[]{:S(2)}) collective-permute-start(bf16[32,32,512]{2,1,0:T(8,128)(2,1)S(1)} %get-tuple-element.24), channel_id=1, source_target_pairs={{0,2},{1,3},{2,4},{3,5},{4,6},{5,7},{6,8},{7,9},{8,10},{9,11},{10,... | collective-permute-start | bytes 3145736 | tf_op jit(solution)/shard_map/ppermute | solution.py:12
  224.9 24.7 %collective-permute-start.7 = (bf16[32,32,512]{2,1,0:T(8,128)(2,1)S(1)}, bf16[32,32,512]{2,1,0:T(8,128)(2,1)S(1)}, u32[]{:S(2)}, u32[]{:S(2)}) collective-permute-start(bf16[32,32,512]{2,1,0:T(8,128)(2,1)S(1)} %fusion.288), channel_id=1, source_target_pairs={{0,4},{1,5},{2,6},{3,7},{4,8},{5,9},{6,10},{7,11},{8,12},{9,13},{1... | collective-permute-start | bytes 3145736 | tf_op jit(solution)/shard_map/ppermute | solution.py:12
  263.0 20.2 %collective-permute-start.8 = (bf16[32,32,512]{2,1,0:T(8,128)(2,1)S(1)}, bf16[32,32,512]{2,1,0:T(8,128)(2,1)S(1)}, u32[]{:S(2)}, u32[]{:S(2)}) collective-permute-start(bf16[32,32,512]{2,1,0:T(8,128)(2,1)S(1)} %get-tuple-element.22), channel_id=1, source_target_pairs={{0,8},{1,9},{2,10},{3,11},{4,12},{5,13},{6,14},{7,15},{8,16},{9,17... | collective-permute-start | bytes 3145736 | tf_op jit(solution)/shard_map/ppermute | solution.py:12
  289.9 21.2 %collective-permute-start.9 = (bf16[32,32,512]{2,1,0:T(8,128)(2,1)S(1)}, bf16[32,32,512]{2,1,0:T(8,128)(2,1)S(1)}, u32[]{:S(2)}, u32[]{:S(2)}) collective-permute-start(bf16[32,32,512]{2,1,0:T(8,128)(2,1)S(1)} %fusion.289), channel_id=1, source_target_pairs={{0,16},{1,17},{2,18},{3,19},{4,20},{5,21},{6,22},{7,23},{8,24},{9,... | collective-permute-start | bytes 3145736 | tf_op jit(solution)/shard_map/ppermute | solution.py:12
  360.1 8.4 collective-permute-start.12
  379.0 9.8 %collective-permute-start.13 = (bf16[32,8,512]{2,1,0:T(8,128)(2,1)S(1)}, bf16[32,8,512]{2,1,0:T(8,128)(2,1)S(1)}, u32[]{:S(2)}, u32[]{:S(2)}) collective-permute-start(bf16[32,8,512]{2,1,0:T(8,128)(2,1)S(1)} %slice.1053), channel_id=1, source_target_pairs={{0,1},{1,2},{2,3},{3,4},{4,5},{5,6},{6,7},{7,8},{8,9},{9,10},{10,1... | collective-permute-start | bytes 786440 | tf_op jit(solution)/shard_map/ppermute | solution.py:12
  399.2 12.6 %collective-permute-start.14 = (bf16[32,16,512]{2,1,0:T(8,128)(2,1)S(1)}, bf16[32,16,512]{2,1,0:T(8,128)(2,1)S(1)}, u32[]{:S(2)}, u32[]{:S(2)}) collective-permute-start(bf16[32,16,512]{2,1,0:T(8,128)(2,1)S(1)} %get-tuple-element.32), channel_id=1, source_target_pairs={{0,1},{1,2},{2,3},{3,4},{4,5},{5,6},{6,7},{7,8},{8,9},{9,10},{10,1... | collective-permute-start | bytes 1572872 | tf_op jit(solution)/shard_map/ppermute | solution.py:12
  421.8 18.2 %collective-permute-start.15 = (bf16[32,32,512]{2,1,0:T(8,128)(2,1)S(1)}, bf16[32,32,512]{2,1,0:T(8,128)(2,1)S(1)}, u32[]{:S(2)}, u32[]{:S(2)}) collective-permute-start(bf16[32,32,512]{2,1,0:T(8,128)(2,1)S(1)} %fusion.292), channel_id=1, source_target_pairs={{0,1},{1,2},{2,3},{3,4},{4,5},{5,6},{6,7},{7,8},{8,9},{9,10},{10,1... | collective-permute-start | bytes 3145736 | tf_op jit(solution)/shard_map/ppermute | solution.py:12
  453.2 25.2 %collective-permute-start.16 = (bf16[32,32,512]{2,1,0:T(8,128)(2,1)S(1)}, bf16[32,32,512]{2,1,0:T(8,128)(2,1)S(1)}, u32[]{:S(2)}, u32[]{:S(2)}) collective-permute-start(bf16[32,32,512]{2,1,0:T(8,128)(2,1)S(1)} %get-tuple-element.14), channel_id=1, source_target_pairs={{0,2},{1,3},{2,4},{3,5},{4,6},{5,7},{6,8},{7,9},{8,10},{9,11},{10,... | collective-permute-start | bytes 3145736 | tf_op jit(solution)/shard_map/ppermute | solution.py:12
  485.2 24.7 %collective-permute-start.17 = (bf16[32,32,512]{2,1,0:T(8,128)(2,1)S(1)}, bf16[32,32,512]{2,1,0:T(8,128)(2,1)S(1)}, u32[]{:S(2)}, u32[]{:S(2)}) collective-permute-start(bf16[32,32,512]{2,1,0:T(8,128)(2,1)S(1)} %fusion.293), channel_id=1, source_target_pairs={{0,4},{1,5},{2,6},{3,7},{4,8},{5,9},{6,10},{7,11},{8,12},{9,13},{1... | collective-permute-start | bytes 3145736 | tf_op jit(solution)/shard_map/ppermute | solution.py:12
  520.8 20.1 %collective-permute-start.18 = (bf16[32,32,512]{2,1,0:T(8,128)(2,1)}, bf16[32,32,512]{2,1,0:T(8,128)(2,1)S(1)}, u32[]{:S(2)}, u32[]{:S(2)}) collective-permute-start(bf16[32,32,512]{2,1,0:T(8,128)(2,1)} %get-tuple-element.12), channel_id=1, source_target_pairs={{0,8},{1,9},{2,10},{3,11},{4,12},{5,13},{6,14},{7,15},{8,16},{9,17... | collective-permute-start | bytes 3145736 | tf_op jit(solution)/shard_map/ppermute | solution.py:12
  547.7 21.2 %collective-permute-start.19 = (bf16[32,32,512]{2,1,0:T(8,128)(2,1)S(1)}, bf16[32,32,512]{2,1,0:T(8,128)(2,1)S(1)}, u32[]{:S(2)}, u32[]{:S(2)}) collective-permute-start(bf16[32,32,512]{2,1,0:T(8,128)(2,1)S(1)} %fusion.294), channel_id=1, source_target_pairs={{0,16},{1,17},{2,18},{3,19},{4,20},{5,21},{6,22},{7,23},{8,24},{9,... | collective-permute-start | bytes 3145736 | tf_op jit(solution)/shard_map/ppermute | solution.py:12
  636.4 9.8 %collective-permute-start.23 = (bf16[32,8,512]{2,1,0:T(8,128)(2,1)S(1)}, bf16[32,8,512]{2,1,0:T(8,128)(2,1)S(1)}, u32[]{:S(2)}, u32[]{:S(2)}) collective-permute-start(bf16[32,8,512]{2,1,0:T(8,128)(2,1)S(1)} %slice.1123), channel_id=1, source_target_pairs={{0,1},{1,2},{2,3},{3,4},{4,5},{5,6},{6,7},{7,8},{8,9},{9,10},{10,1... | collective-permute-start | bytes 786440 | tf_op jit(solution)/shard_map/ppermute | solution.py:12
  656.5 12.6 %collective-permute-start.24 = (bf16[32,16,512]{2,1,0:T(8,128)(2,1)S(1)}, bf16[32,16,512]{2,1,0:T(8,128)(2,1)S(1)}, u32[]{:S(2)}, u32[]{:S(2)}) collective-permute-start(bf16[32,16,512]{2,1,0:T(8,128)(2,1)S(1)} %get-tuple-element.30), channel_id=1, source_target_pairs={{0,1},{1,2},{2,3},{3,4},{4,5},{5,6},{6,7},{7,8},{8,9},{9,10},{10,1... | collective-permute-start | bytes 1572872 | tf_op jit(solution)/shard_map/ppermute | solution.py:12
  679.3 18.2 %collective-permute-start.25 = (bf16[32,32,512]{2,1,0:T(8,128)(2,1)S(1)}, bf16[32,32,512]{2,1,0:T(8,128)(2,1)S(1)}, u32[]{:S(2)}, u32[]{:S(2)}) collective-permute-start(bf16[32,32,512]{2,1,0:T(8,128)(2,1)S(1)} %fusion.297), channel_id=1, source_target_pairs={{0,1},{1,2},{2,3},{3,4},{4,5},{5,6},{6,7},{7,8},{8,9},{9,10},{10,1... | collective-permute-start | bytes 3145736 | tf_op jit(solution)/shard_map/ppermute | solution.py:12
  711.6 25.2 %collective-permute-start.26 = (bf16[32,32,512]{2,1,0:T(8,128)(2,1)}, bf16[32,32,512]{2,1,0:T(8,128)(2,1)S(1)}, u32[]{:S(2)}, u32[]{:S(2)}) collective-permute-start(bf16[32,32,512]{2,1,0:T(8,128)(2,1)} %get-tuple-element.4), channel_id=1, source_target_pairs={{0,2},{1,3},{2,4},{3,5},{4,6},{5,7},{6,8},{7,9},{8,10},{9,11},{10,... | collective-permute-start | bytes 3145736 | tf_op jit(solution)/shard_map/ppermute | solution.py:12
  743.6 24.7 %collective-permute-start.27 = (bf16[32,32,512]{2,1,0:T(8,128)(2,1)S(1)}, bf16[32,32,512]{2,1,0:T(8,128)(2,1)S(1)}, u32[]{:S(2)}, u32[]{:S(2)}) collective-permute-start(bf16[32,32,512]{2,1,0:T(8,128)(2,1)S(1)} %fusion.298), channel_id=1, source_target_pairs={{0,4},{1,5},{2,6},{3,7},{4,8},{5,9},{6,10},{7,11},{8,12},{9,13},{1... | collective-permute-start | bytes 3145736 | tf_op jit(solution)/shard_map/ppermute | solution.py:12
  778.3 20.2 %collective-permute-start.28 = (bf16[32,32,512]{2,1,0:T(8,128)(2,1)S(1)}, bf16[32,32,512]{2,1,0:T(8,128)(2,1)S(1)}, u32[]{:S(2)}, u32[]{:S(2)}) collective-permute-start(bf16[32,32,512]{2,1,0:T(8,128)(2,1)S(1)} %get-tuple-element.2), channel_id=1, source_target_pairs={{0,8},{1,9},{2,10},{3,11},{4,12},{5,13},{6,14},{7,15},{8,16},{9,17... | collective-permute-start | bytes 3145736 | tf_op jit(solution)/shard_map/ppermute | solution.py:12
  807.3 21.2 %collective-permute-start.29 = (bf16[32,32,512]{2,1,0:T(8,128)(2,1)S(1)}, bf16[32,32,512]{2,1,0:T(8,128)(2,1)S(1)}, u32[]{:S(2)}, u32[]{:S(2)}) collective-permute-start(bf16[32,32,512]{2,1,0:T(8,128)(2,1)S(1)} %fusion.299), channel_id=1, source_target_pairs={{0,16},{1,17},{2,18},{3,19},{4,20},{5,21},{6,22},{7,23},{8,24},{9,... | collective-permute-start | bytes 3145736 | tf_op jit(solution)/shard_map/ppermute | solution.py:12
  (31 other events, 268.6 us)
where the time goes:
time: 859 us; the launch traced here: 848 us
  waiting for transfers between devices  361 us (42%)
  matrix products  269 us (31%)
  local copies, waits for them, and re-layouts  87.6 us (10%)
  other arithmetic  68.3 us (8%)
  starting transfers between devices  60.2 us (7%)
    ppermute x30, waiting for transfers between devices, move_right(): lax.ppermute(block, SEQ_AXES, perm=[(source, source + hops) for source in...  361 us
    dot_general x30, matrix products, gated_layer(): jnp.einsum('bsc,cd->bsd', activated, w_out, preferred_element_type=jnp.fl...  122 us
    dot_general x30, matrix products, gated_layer(): jnp.einsum('bsc,cd->bsd', delayed, w_del, preferred_element_type=jnp.floa...  106 us
    ppermute x30, starting transfers between devices, move_right(): lax.ppermute(block, SEQ_AXES, perm=[(source, source + hops) for source in...  60.2 us
    convert_element_type x29, other arithmetic, local_stack(): current = residual.astype(jnp.bfloat16)  53.9 us
    unnamed x53, local copies, waits for them, and re-layouts  53.5 us
    dot_general x30, matrix products, gated_layer(): jnp.einsum('bsc,cd->bsd', current, w_cur, preferred_element_type=jnp.floa...  41.2 us
  transfers between devices with their start and end apart: 30, of which 29 were waited for; matrix products, arithmetic and copies ran while one was open for 12% of the time, Pallas kernels for 0%

commit v1 on v0

v1 whole, which is shorter than its diff:
```python
import functools

import jax
import jax.numpy as jnp
from jax import lax
from jax.experimental import pallas as pl
from jax.experimental.pallas import tpu as pltpu
from jax.sharding import PartitionSpec as P

SEQ_AXES = ("seq_hi", "seq")
MESH = pl.DeviceIdType.MESH

TEAM = 2
ROW_TILE = 256
COL_TILE = 256
ALIGN = 16
N_BUF = 5
AHEAD = N_BUF - 1


def halo_layout(n_cyc):
    sizes = [max(2 ** cyc, ALIGN) for cyc in range(n_cyc)]
    starts = [sum(sizes[:cyc]) for cyc in range(n_cyc)]
    return starts, sizes, sum(sizes)


def stack_kernel(n_hi, n_lo, n_rep, n_cyc, x_ref, wf0_ref, wf1_ref, wg0_ref, wg1_ref, wr_ref, ws_ref, h_out, skip_out,
                 x_buf, h_acc, skip_acc, u_buf, halo, w_sq, w_sk,
                 w_sem, x_send, x_recv, halo_send, halo_recv, h_send, h_recv, s_send, s_recv):
    n_dev = n_hi * n_lo
    block_len, chans = x_ref.shape[1], x_ref.shape[2]
    skip_ch = skip_out.shape[2]
    part_rows = h_acc.shape[1]
    per_part = n_dev // TEAM
    half_starts, halo_sizes, _ = halo_layout(n_cyc)
    n_layers = n_rep * n_cyc

    group = lax.axis_index("batch")
    me = lax.axis_index("seq_hi") * n_lo + lax.axis_index("seq")
    team = me // TEAM
    part = me % TEAM

    def device(index):
        return (group, index // n_lo, index % n_lo)

    squares = (wf0_ref, wf1_ref, wg0_ref, wg1_ref, wr_ref)

    def weight_copies(rep, cyc):
        slot = cyc % N_BUF
        copies = [pltpu.make_async_copy(ref.at[rep, cyc], w_sq.at[slot, i], w_sem.at[slot, i]) for i, ref in enumerate(squares)]
        copies.append(pltpu.make_async_copy(ws_ref.at[rep, cyc], w_sk.at[slot], w_sem.at[slot, len(squares)]))
        return copies

    for cyc in range(AHEAD):
        for copy in weight_copies(0, cyc):
            copy.start()

    barrier = pltpu.get_barrier_semaphore()

    def greet(index, _):
        @pl.when(index != me)
        def _():
            pl.semaphore_signal(barrier, inc=1, device_id=device(index), device_id_type=MESH)
        return 0

    lax.fori_loop(0, n_dev, greet, 0)
    pl.semaphore_wait(barrier, n_dev - 1)

    def x_target(step):
        to_team = (team + step) % per_part
        return to_team, to_team * TEAM + me // per_part

    def x_copies(seq, to_team, target, remote):
        src = x_ref.at[to_team * TEAM + seq]
        place = me % per_part
        dst = x_buf.at[seq, pl.ds(place * block_len, block_len)]
        if remote:
            return pltpu.make_async_remote_copy(src_ref=src, dst_ref=dst, send_sem=x_send.at[seq, to_team], recv_sem=x_recv.at[seq, place],
                                                device_id=device(target), device_id_type=MESH)
        return pltpu.make_async_copy(src, dst, x_recv.at[seq, place])

    for seq in range(TEAM):
        def send_x(step, _, seq=seq):
            to_team, target = x_target(step)

            @pl.when(target != me)
            def _():
                x_copies(seq, to_team, target, True).start()

            @pl.when(target == me)
            def _():
                x_copies(seq, to_team, target, False).start()
            return 0

        lax.fori_loop(0, per_part, send_x, 0)

    zero_slot = TEAM * n_rep
    halo[zero_slot] = jnp.zeros(halo.shape[1:], halo.dtype)

    def halo_copy(slot, cyc):
        size = halo_sizes[cyc]
        return pltpu.make_async_remote_copy(
            src_ref=u_buf.at[cyc % 2, pl.ds(part_rows - size, size)],
            dst_ref=halo.at[slot, pl.ds(half_starts[cyc], size)],
            send_sem=halo_send.at[cyc % 2],
            recv_sem=halo_recv.at[slot, cyc],
            device_id=device(team * TEAM + (TEAM - 1)),
            device_id_type=MESH,
        )

    n_tiles = part_rows // ROW_TILE

    def delayed_tile(cyc, tile, read_slot):
        dil = 2 ** cyc
        first = tile * ROW_TILE
        start = half_starts[cyc]
        cur = u_buf.at[cyc % 2]
        if dil % ALIGN == 0:
            if first + ROW_TILE <= dil:
                return halo[read_slot, pl.ds(start + first, ROW_TILE), :]
            if first >= dil:
                return cur[pl.ds(first - dil, ROW_TILE), :]
            return jnp.concatenate([halo[read_slot, pl.ds(start + first, dil - first), :], cur[pl.ds(0, ROW_TILE - dil + first), :]], axis=0)
        if first == 0:
            before = halo[read_slot, pl.ds(start, ALIGN), :]
        else:
            before = cur[pl.ds(first - ALIGN, ALIGN), :]
        both = jnp.concatenate([before, cur[pl.ds(first, ROW_TILE), :]], axis=0).astype(jnp.float32)
        return pltpu.roll(both, dil, 0)[ALIGN:].astype(jnp.bfloat16)

    def dot(left, right):
        return jnp.dot(left, right, preferred_element_type=jnp.float32)

    def layer(seq, rep, cyc):
        wslot = cyc % N_BUF
        slot = seq * n_rep + rep
        read_slot = jnp.where(part == 0, zero_slot, slot)

        for copy in weight_copies(rep, cyc):
            copy.wait()
        nxt_cyc = (cyc + AHEAD) % n_cyc
        nxt_rep = rep + (cyc + AHEAD) // n_cyc

        @pl.when(jnp.logical_or(nxt_rep < n_rep, seq + 1 < TEAM))
        def _():
            for copy in weight_copies(nxt_rep % n_rep, nxt_cyc):
                copy.start()

        @pl.when(part == 0)
        def _():
            halo_copy(slot, cyc).start()

        @pl.when(part == TEAM - 1)
        def _():
            halo_copy(slot, cyc).wait_recv()

        cur, nxt = u_buf.at[cyc % 2], u_buf.at[(cyc + 1) % 2]
        acts = []
        for tile in range(n_tiles):
            rows = pl.ds(tile * ROW_TILE, ROW_TILE)
            now = cur[rows, :]
            before = delayed_tile(cyc, tile, read_slot)
            pieces = []
            for col in range(0, chans, COL_TILE):
                cols = pl.ds(col, COL_TILE)
                f = dot(now, w_sq[wslot, 1, :, cols]) + dot(before, w_sq[wslot, 0, :, cols])
                g = dot(now, w_sq[wslot, 3, :, cols]) + dot(before, w_sq[wslot, 2, :, cols])
                pieces.append((jnp.tanh(f) * (0.5 * jnp.tanh(0.5 * g) + 0.5)).astype(jnp.bfloat16))
            acts.append(jnp.concatenate(pieces, axis=1))
        for tile in range(n_tiles):
            rows = pl.ds(tile * ROW_TILE, ROW_TILE)
            for col in range(0, chans, COL_TILE):
                cols = pl.ds(col, COL_TILE)
                new = h_acc[seq, rows, cols] + dot(acts[tile], w_sq[wslot, 4, :, cols])
                h_acc[seq, rows, cols] = new
                nxt[rows, cols] = new.astype(jnp.bfloat16)
            skip_acc[seq, rows, :] += dot(acts[tile], w_sk[wslot])

        @pl.when(part == 0)
        def _():
            halo_copy(slot, cyc).wait_send()

    def out_copies(seq, step, remote):
        place = (me + step) % per_part
        target = part * per_part + place
        rows = pl.ds(place * block_len, block_len)
        which = team * TEAM + seq
        pairs = ((h_acc, h_out, h_send, h_recv), (skip_acc, skip_out, s_send, s_recv))
        if remote:
            return target, [pltpu.make_async_remote_copy(src_ref=acc.at[seq, rows], dst_ref=out.at[which], send_sem=send.at[seq, place],
                                                         recv_sem=recv.at[seq, team], device_id=device(target), device_id_type=MESH)
                            for acc, out, send, recv in pairs]
        return target, [pltpu.make_async_copy(acc.at[seq, rows], out.at[which], recv.at[seq, team]) for acc, out, send, recv in pairs]

    def one_sequence(seq, _):
        def wait_x(place, _):
            dst = x_buf.at[seq, pl.ds(place * block_len, block_len)]
            pltpu.make_async_copy(dst, dst, x_recv.at[seq, place]).wait()
            return 0

        lax.fori_loop(0, per_part, wait_x, 0)
        start = x_buf[seq]
        u_buf[0] = start
        h_acc[seq] = start.astype(jnp.float32)
        skip_acc[seq] = jnp.zeros(skip_acc.shape[1:], jnp.float32)

        def one_cycle(rep, _):
            for cyc in range(n_cyc):
                layer(seq, rep, cyc)
            return 0

        lax.fori_loop(0, n_rep, one_cycle, 0)

        def send_out(step, _):
            target, copies = out_copies(seq, step, True)

            @pl.when(target != me)
            def _():
                for copy in copies:
                    copy.start()

            @pl.when(target == me)
            def _():
                for copy in out_copies(seq, step, False)[1]:
                    copy.start()
            return 0

        lax.fori_loop(0, per_part, send_out, 0)
        return 0

    lax.fori_loop(0, TEAM, one_sequence, 0)

    for seq in range(TEAM):
        def finish(step, _, seq=seq):
            to_team, target = x_target(step)

            @pl.when(target != me)
            def _():
                x_copies(seq, to_team, target, True).wait_send()
            target, copies = out_copies(seq, step, True)

            @pl.when(target != me)
            def _():
                for copy in copies:
                    copy.wait_send()
            dst = h_out.at[step * TEAM + seq]
            pltpu.make_async_copy(dst, dst, h_recv.at[seq, step]).wait()
            dst = skip_out.at[step * TEAM + seq]
            pltpu.make_async_copy(dst, dst, s_recv.at[seq, step]).wait()
            return 0

        lax.fori_loop(0, per_part, finish, 0)


def solution(mesh):
    n_hi, n_lo = mesh.shape["seq_hi"], mesh.shape["seq"]
    n_dev = n_hi * n_lo
    seq_spec = P("batch", SEQ_AXES, None)

    def local_stack(x_loc, w_f0, w_f1, w_g0, w_g1, w_res, w_skip):
        n_seq, block_len, chans = x_loc.shape
        n_rep, n_cyc, skip_ch = w_f0.shape[0], w_f0.shape[1], w_skip.shape[-1]
        assert n_seq == n_dev and n_dev % TEAM == 0 and n_cyc % N_BUF == 0 and n_cyc % 2 == 0
        part_rows = n_dev * block_len // TEAM
        per_part = n_dev // TEAM
        assert part_rows >= 2 ** (n_cyc - 1) and part_rows % ROW_TILE == 0
        halo_rows = halo_layout(n_cyc)[2]
        sem = pltpu.SemaphoreType.DMA
        return pl.pallas_call(
            functools.partial(stack_kernel, n_hi, n_lo, n_rep, n_cyc),
            out_shape=(jax.ShapeDtypeStruct((n_seq, block_len, chans), jnp.float32),
                       jax.ShapeDtypeStruct((n_seq, block_len, skip_ch), jnp.float32)),
            in_specs=[pl.BlockSpec(memory_space=pl.ANY)] * 7,
            out_specs=(pl.BlockSpec(memory_space=pl.ANY),) * 2,
            scratch_shapes=[
                pltpu.VMEM((TEAM, part_rows, chans), jnp.bfloat16),
                pltpu.VMEM((TEAM, part_rows, chans), jnp.float32),
                pltpu.VMEM((TEAM, part_rows, skip_ch), jnp.float32),
                pltpu.VMEM((2, part_rows, chans), jnp.bfloat16),
                pltpu.VMEM((TEAM * n_rep + 1, halo_rows, chans), jnp.bfloat16),
                pltpu.VMEM((N_BUF, 5, chans, chans), jnp.bfloat16),
                pltpu.VMEM((N_BUF, chans, skip_ch), jnp.bfloat16),
                sem((N_BUF, 6)),
                sem((TEAM, per_part)),
                sem((TEAM, per_part)),
                sem((2,)),
                sem((TEAM * n_rep, n_cyc)),
                sem((TEAM, per_part)),
                sem((TEAM, per_part)),
                sem((TEAM, per_part)),
                sem((TEAM, per_part)),
            ],
            compiler_params=pltpu.CompilerParams(collective_id=0, has_side_effects=True, vmem_limit_bytes=60 * 1024 * 1024),
        )(x_loc, w_f0, w_f1, w_g0, w_g1, w_res, w_skip)

    return jax.shard_map(local_stack, mesh=mesh, in_specs=(seq_spec, P(), P(), P(), P(), P(), P()), out_specs=(seq_spec, seq_spec), check_vma=False)
```

time: 859 us -> 153 us (0.18)
  the two profiles are of different devices: /device:TPU:120 before, /device:TPU:113 now
where the time goes in v1:
time: 153 us
  Pallas kernels  147 us (96%)
  local copies, waits for them, and re-layouts  5.49 us (4%)
    pallas_call x1, Pallas kernels, local_stack(): pl.pallas_call(functools.partial(stack_kernel, n_hi, n_lo, n_rep, n_cyc),...  147 us
    unnamed x2, local copies, waits for them, and re-layouts  5.49 us

profile of v1, /device:TPU:113, one launch (start us, length us, event | category | flops | bytes accessed | tf_op | source)
XLA Modules:
  0.0 153.1 jit_solution(17110313535469534303)
XLA Ops:
  0.6 147.0 %shard_map.86 = (f32[32,32,512]{2,1,0:T(8,128)}, f32[32,32,256]{2,1,0:T(8,128)}) custom-call(bf16[32,32,512]{2,1,0:T(8,128)(2,1)} %x_ref.1, bf16[3,10,512,512]{3,2,1,0:T(8,128)(2,1)} %wf0_ref.1, bf16[3,10,512,512]{3,2,1,0:T(8,128)(2,1)} %wf1_ref.1, bf16[3,10,512,512]{3,2,1,0:T(8,128)(2,1)} %wg0_ref.1, bf16[3,10,512,512]{3,2,1,0:T(8,128)(2,1)} %wg1_ref.1, ...), custom_call_target="tpu_custom_call" | custom-call | tf_op jit(solution)/shard_map/pallas_call | solution.py:269
  147.6 3.2 %copy.11 = f32[32,32,512]{2,1,0:T(8,128)} copy(f32[32,32,512]{2,1,0:T(8,128)} %get-tuple-element.4) | data formatting | bytes 4194304
  150.8 2.3 %copy.12 = f32[32,32,256]{2,1,0:T(8,128)} copy(f32[32,32,256]{2,1,0:T(8,128)} %get-tuple-element.5) | data formatting | bytes 2097152

commit v2 on v1

--- a/solution.py
+++ b/solution.py
@@ -14,8 +14,9 @@
 ROW_TILE = 256
 COL_TILE = 256
 ALIGN = 16
-N_BUF = 5
-AHEAD = N_BUF - 1
+GROUP = 2
+U_BUF = 5
+FIRST = 4
 
 
 def halo_layout(n_cyc):
@@ -46,14 +47,17 @@
     squares = (wf0_ref, wf1_ref, wg0_ref, wg1_ref, wr_ref)
 
     def weight_copies(rep, cyc):
-        slot = cyc % N_BUF
+        slot = cyc
         copies = [pltpu.make_async_copy(ref.at[rep, cyc], w_sq.at[slot, i], w_sem.at[slot, i]) for i, ref in enumerate(squares)]
         copies.append(pltpu.make_async_copy(ws_ref.at[rep, cyc], w_sk.at[slot], w_sem.at[slot, len(squares)]))
         return copies
 
-    for cyc in range(AHEAD):
-        for copy in weight_copies(0, cyc):
-            copy.start()
+    def first_weights(start, end):
+        for cyc in range(start, end):
+            for copy in weight_copies(0, cyc):
+                copy.start()
+
+    first_weights(0, FIRST)
 
     barrier = pltpu.get_barrier_semaphore()
 
@@ -79,8 +83,8 @@
                                                 device_id=device(target), device_id_type=MESH)
         return pltpu.make_async_copy(src, dst, x_recv.at[seq, place])
 
-    for seq in range(TEAM):
-        def send_x(step, _, seq=seq):
+    def send_all_x(seq):
+        def send_x(step, _):
             to_team, target = x_target(step)
 
             @pl.when(target != me)
@@ -94,15 +98,17 @@
 
         lax.fori_loop(0, per_part, send_x, 0)
 
+    send_all_x(0)
+    first_weights(FIRST, n_cyc - GROUP)
     zero_slot = TEAM * n_rep
     halo[zero_slot] = jnp.zeros(halo.shape[1:], halo.dtype)
 
     def halo_copy(slot, cyc):
         size = halo_sizes[cyc]
         return pltpu.make_async_remote_copy(
-            src_ref=u_buf.at[cyc % 2, pl.ds(part_rows - size, size)],
+            src_ref=u_buf.at[cyc % U_BUF, pl.ds(part_rows - size, size)],
             dst_ref=halo.at[slot, pl.ds(half_starts[cyc], size)],
-            send_sem=halo_send.at[cyc % 2],
+            send_sem=halo_send.at[cyc],
             recv_sem=halo_recv.at[slot, cyc],
             device_id=device(team * TEAM + (TEAM - 1)),
             device_id_type=MESH,
@@ -114,7 +120,7 @@
         dil = 2 ** cyc
         first = tile * ROW_TILE
         start = half_starts[cyc]
-        cur = u_buf.at[cyc % 2]
+        cur = u_buf.at[cyc % U_BUF]
         if dil % ALIGN == 0:
             if first + ROW_TILE <= dil:
                 return halo[read_slot, pl.ds(start + first, ROW_TILE), :]
@@ -131,30 +137,67 @@
     def dot(left, right):
         return jnp.dot(left, right, preferred_element_type=jnp.float32)
 
+    def sent_at(first):
+        return range(max(first - GROUP + 1, 0), min(first + 1, n_cyc))
+
+    def stop(seq, rep, first):
+        slot = seq * n_rep + rep
+
+        def weights(cyc, act):
+            at_rep = rep + cyc // n_cyc
+            copies = weight_copies(at_rep % n_rep, cyc % n_cyc)
+            if cyc < n_cyc:
+                for copy in copies:
+                    act(copy)
+            else:
+                @pl.when(jnp.logical_or(at_rep < n_rep, seq + 1 < TEAM))
+                def _():
+                    for copy in copies:
+                        act(copy)
+
+        @pl.when(part == 0)
+        def _():
+            for cyc in sent_at(first):
+                halo_copy(slot, cyc).start()
+
+        for cyc in range(first + n_cyc - GROUP, first + n_cyc):
+            weights(cyc, lambda copy: copy.start())
+
+        if first < n_cyc:
+            before = first - GROUP
+            gone = list(sent_at(before)) if before >= 0 else []
+            gone_prev = list(sent_at(before + n_cyc)) if before < 0 else list(sent_at(n_cyc)) if before == 0 else []
+
+            @pl.when(part == 0)
+            def _():
+                for cyc in gone:
+                    halo_copy(slot, cyc).wait_send()
+
+            @pl.when(jnp.logical_and(part == 0, slot > 0))
+            def _():
+                for cyc in gone_prev:
+                    halo_copy(slot, cyc).wait_send()
+
+            for cyc in range(first + GROUP, first + 2 * GROUP):
+                weights(cyc, lambda copy: copy.wait())
+
+            @pl.when(part == TEAM - 1)
+            def _():
+                for cyc in range(first, first + GROUP):
+                    halo_copy(slot, cyc).wait_recv()
+
+    def cycle_end(seq, rep):
+        if GROUP > 1:
+            @pl.when(part == 0)
+            def _():
+                for cyc in range(n_cyc - GROUP + 1, n_cyc):
+                    halo_copy(seq * n_rep + rep, cyc).start()
+
+
     def layer(seq, rep, cyc):
-        wslot = cyc % N_BUF
         slot = seq * n_rep + rep
         read_slot = jnp.where(part == 0, zero_slot, slot)
-
-        for copy in weight_copies(rep, cyc):
-            copy.wait()
-        nxt_cyc = (cyc + AHEAD) % n_cyc
-        nxt_rep = rep + (cyc + AHEAD) // n_cyc
-
-        @pl.when(jnp.logical_or(nxt_rep < n_rep, seq + 1 < TEAM))
-        def _():
-            for copy in weight_copies(nxt_rep % n_rep, nxt_cyc):
-                copy.start()
-
-        @pl.when(part == 0)
-        def _():
-            halo_copy(slot, cyc).start()
-
-        @pl.when(part == TEAM - 1)
-        def _():
-            halo_copy(slot, cyc).wait_recv()
-
-        cur, nxt = u_buf.at[cyc % 2], u_buf.at[(cyc + 1) % 2]
+        cur, nxt = u_buf.at[cyc % U_BUF], u_buf.at[(cyc + 1) % U_BUF]
         acts = []
         for tile in range(n_tiles):
             rows = pl.ds(tile * ROW_TILE, ROW_TILE)
@@ -163,25 +206,21 @@
             pieces = []
             for col in range(0, chans, COL_TILE):
                 cols = pl.ds(col, COL_TILE)
-                f = dot(now, w_sq[wslot, 1, :, cols]) + dot(before, w_sq[wslot, 0, :, cols])
-                g = dot(now, w_sq[wslot, 3, :, cols]) + dot(before, w_sq[wslot, 2, :, cols])
+                f = dot(now, w_sq[cyc, 1, :, cols]) + dot(before, w_sq[cyc, 0, :, cols])
+                g = dot(now, w_sq[cyc, 3, :, cols]) + dot(before, w_sq[cyc, 2, :, cols])
                 pieces.append((jnp.tanh(f) * (0.5 * jnp.tanh(0.5 * g) + 0.5)).astype(jnp.bfloat16))
             acts.append(jnp.concatenate(pieces, axis=1))
         for tile in range(n_tiles):
             rows = pl.ds(tile * ROW_TILE, ROW_TILE)
             for col in range(0, chans, COL_TILE):
                 cols = pl.ds(col, COL_TILE)
-                new = h_acc[seq, rows, cols] + dot(acts[tile], w_sq[wslot, 4, :, cols])
+                new = h_acc[seq, rows, cols] + dot(acts[tile], w_sq[cyc, 4, :, cols])
                 h_acc[seq, rows, cols] = new
                 nxt[rows, cols] = new.astype(jnp.bfloat16)
-            skip_acc[seq, rows, :] += dot(acts[tile], w_sk[wslot])
-
-        @pl.when(part == 0)
-        def _():
-            halo_copy(slot, cyc).wait_send()
+            skip_acc[seq, rows, :] += dot(acts[tile], w_sk[cyc])
 
     def out_copies(seq, step, remote):
-        place = (me + step) % per_part
+        place = (2 * ((me // 2 + step) % (per_part // 2)) + step // (per_part // 2)) % per_part
         target = part * per_part + place
         rows = pl.ds(place * block_len, block_len)
         which = team * TEAM + seq
@@ -192,21 +231,29 @@
                             for acc, out, send, recv in pairs]
         return target, [pltpu.make_async_copy(acc.at[seq, rows], out.at[which], recv.at[seq, team]) for acc, out, send, recv in pairs]
 
+    def wait_x(seq, place, _):
+        dst = x_buf.at[seq, pl.ds(place * block_len, block_len)]
+        pltpu.make_async_copy(dst, dst, x_recv.at[seq, place]).wait()
+        return 0
+
+    early = per_part // 2
+    lax.fori_loop(0, early, functools.partial(wait_x, 0), 0)
+    for seq in range(1, TEAM):
+        send_all_x(seq)
+
     def one_sequence(seq, _):
-        def wait_x(place, _):
-            dst = x_buf.at[seq, pl.ds(place * block_len, block_len)]
-            pltpu.make_async_copy(dst, dst, x_recv.at[seq, place]).wait()
-            return 0
-
-        lax.fori_loop(0, per_part, wait_x, 0)
+        lax.fori_loop(jnp.where(seq == 0, early, 0), per_part, functools.partial(wait_x, seq), 0)
         start = x_buf[seq]
         u_buf[0] = start
         h_acc[seq] = start.astype(jnp.float32)
         skip_acc[seq] = jnp.zeros(skip_acc.shape[1:], jnp.float32)
 
         def one_cycle(rep, _):
-            for cyc in range(n_cyc):
-                layer(seq, rep, cyc)
+            for first in range(0, n_cyc, GROUP):
+                stop(seq, rep, first)
+                for cyc in range(first, first + GROUP):
+                    layer(seq, rep, cyc)
+            cycle_end(seq, rep)
             return 0
 
         lax.fori_loop(0, n_rep, one_cycle, 0)
@@ -228,7 +275,15 @@
         lax.fori_loop(0, per_part, send_out, 0)
         return 0
 
+    for cyc in range(GROUP):
+        for copy in weight_copies(0, cyc):
+            copy.wait()
     lax.fori_loop(0, TEAM, one_sequence, 0)
+
+    @pl.when(part == 0)
+    def _():
+        for cyc in range(n_cyc - 2 * GROUP + 1, n_cyc):
+            halo_copy(0, cyc).wait_send()
 
     for seq in range(TEAM):
         def finish(step, _, seq=seq):
@@ -260,7 +315,7 @@
     def local_stack(x_loc, w_f0, w_f1, w_g0, w_g1, w_res, w_skip):
         n_seq, block_len, chans = x_loc.shape
         n_rep, n_cyc, skip_ch = w_f0.shape[0], w_f0.shape[1], w_skip.shape[-1]
-        assert n_seq == n_dev and n_dev % TEAM == 0 and n_cyc % N_BUF == 0 and n_cyc % 2 == 0
+        assert n_seq == n_dev and n_dev % TEAM == 0 and n_cyc % GROUP == 0 and n_cyc % U_BUF == 0
         part_rows = n_dev * block_len // TEAM
         per_part = n_dev // TEAM
         assert part_rows >= 2 ** (n_cyc - 1) and part_rows % ROW_TILE == 0
@@ -268,29 +323,28 @@
         sem = pltpu.SemaphoreType.DMA
         return pl.pallas_call(
             functools.partial(stack_kernel, n_hi, n_lo, n_rep, n_cyc),
-            out_shape=(jax.ShapeDtypeStruct((n_seq, block_len, chans), jnp.float32),
-                       jax.ShapeDtypeStruct((n_seq, block_len, skip_ch), jnp.float32)),
+            out_shape=(pltpu.VMEM((n_seq, block_len, chans), jnp.float32), pltpu.VMEM((n_seq, block_len, skip_ch), jnp.float32)),
             in_specs=[pl.BlockSpec(memory_space=pl.ANY)] * 7,
-            out_specs=(pl.BlockSpec(memory_space=pl.ANY),) * 2,
+            out_specs=(pl.BlockSpec(memory_space=pltpu.VMEM),) * 2,
             scratch_shapes=[
                 pltpu.VMEM((TEAM, part_rows, chans), jnp.bfloat16),
                 pltpu.VMEM((TEAM, part_rows, chans), jnp.float32),
                 pltpu.VMEM((TEAM, part_rows, skip_ch), jnp.float32),
-                pltpu.VMEM((2, part_rows, chans), jnp.bfloat16),
+                pltpu.VMEM((U_BUF, part_rows, chans), jnp.bfloat16),
                 pltpu.VMEM((TEAM * n_rep + 1, halo_rows, chans), jnp.bfloat16),
-                pltpu.VMEM((N_BUF, 5, chans, chans), jnp.bfloat16),
-                pltpu.VMEM((N_BUF, chans, skip_ch), jnp.bfloat16),
-                sem((N_BUF, 6)),
-                sem((TEAM, per_part)),
-                sem((TEAM, per_part)),
-                sem((2,)),
+                pltpu.VMEM((n_cyc, 5, chans, chans), jnp.bfloat16),
+                pltpu.VMEM((n_cyc, chans, skip_ch), jnp.bfloat16),
+                sem((n_cyc, 6)),
+                sem((TEAM, per_part)),
+                sem((TEAM, per_part)),
+                sem((n_cyc,)),
                 sem((TEAM * n_rep, n_cyc)),
                 sem((TEAM, per_part)),
                 sem((TEAM, per_part)),
                 sem((TEAM, per_part)),
                 sem((TEAM, per_part)),
             ],
-            compiler_params=pltpu.CompilerParams(collective_id=0, has_side_effects=True, vmem_limit_bytes=60 * 1024 * 1024),
+            compiler_params=pltpu.CompilerParams(collective_id=0, has_side_effects=True, vmem_limit_bytes=52 * 1024 * 1024),
         )(x_loc, w_f0, w_f1, w_g0, w_g1, w_res, w_skip)
 
     return jax.shard_map(local_stack, mesh=mesh, in_specs=(seq_spec, P(), P(), P(), P(), P(), P()), out_specs=(seq_spec, seq_spec), check_vma=False)

time: 153 us -> 146 us (0.954)
  the two profiles are of different devices: /device:TPU:113 before, /device:TPU:105 now
where the time goes in v2:
time: 146 us
  Pallas kernels  143 us (98%)
  local copies, waits for them, and re-layouts  2.29 us (2%)
    pallas_call x1, Pallas kernels, local_stack(): pl.pallas_call(functools.partial(stack_kernel, n_hi, n_lo, n_rep, n_cyc),...  143 us

profile of v2, /device:TPU:105, one launch (start us, length us, event | category | flops | bytes accessed | tf_op | source)
XLA Modules:
  0.0 146.1 jit_solution(824163126359265466)
XLA Ops:
  0.6 143.2 %shard_map.86 = (f32[32,32,512]{2,1,0:T(8,128)S(1)}, f32[32,32,256]{2,1,0:T(8,128)S(1)}) custom-call(bf16[32,32,512]{2,1,0:T(8,128)(2,1)} %x_ref.1, bf16[3,10,512,512]{3,2,1,0:T(8,128)(2,1)} %wf0_ref.1, bf16[3,10,512,512]{3,2,1,0:T(8,128)(2,1)} %wf1_ref.1, bf16[3,10,512,512]{3,2,1,0:T(8,128)(2,1)} %wg0_ref.1, bf16[3,10,512,512]{3,2,1,0:T(8,128)(2,1)} %wg1_ref.1, ...), custom_call_target="tpu_custom_call" | custom-call | tf_op jit(solution)/shard_map/pallas_call | solution.py:324
  143.8 1.3 copy.11
  145.1 1.0 copy.12

commit v3 on v2

--- a/solution.py
+++ b/solution.py
@@ -16,7 +16,7 @@
 ALIGN = 16
 GROUP = 2
 U_BUF = 5
-FIRST = 4
+FIRST = 2
 
 
 def halo_layout(n_cyc):
@@ -48,9 +48,12 @@
 
     def weight_copies(rep, cyc):
         slot = cyc
-        copies = [pltpu.make_async_copy(ref.at[rep, cyc], w_sq.at[slot, i], w_sem.at[slot, i]) for i, ref in enumerate(squares)]
-        copies.append(pltpu.make_async_copy(ws_ref.at[rep, cyc], w_sk.at[slot], w_sem.at[slot, len(squares)]))
+        copies = [pltpu.make_async_copy(ref.at[rep, cyc], w_sq.at[slot, i], w_sem.at[slot, 0]) for i, ref in enumerate(squares)]
+        copies.append(pltpu.make_async_copy(ws_ref.at[rep, cyc], w_sk.at[slot], w_sem.at[slot, 1]))
         return copies
+
+    def weight_waits(cyc):
+        return [pltpu.make_async_copy(buf.at[cyc], buf.at[cyc], w_sem.at[cyc, i]) for i, buf in enumerate((w_sq, w_sk))]
 
     def first_weights(start, end):
         for cyc in range(start, end):
@@ -143,9 +146,10 @@
     def stop(seq, rep, first):
         slot = seq * n_rep + rep
 
-        def weights(cyc, act):
+        def weights(cyc, start):
             at_rep = rep + cyc // n_cyc
-            copies = weight_copies(at_rep % n_rep, cyc % n_cyc)
+            copies = weight_copies(at_rep % n_rep, cyc % n_cyc) if start else weight_waits(cyc % n_cyc)
+            act = (lambda copy: copy.start()) if start else (lambda copy: copy.wait())
             if cyc < n_cyc:
                 for copy in copies:
                     act(copy)
@@ -161,7 +165,7 @@
                 halo_copy(slot, cyc).start()
 
         for cyc in range(first + n_cyc - GROUP, first + n_cyc):
-            weights(cyc, lambda copy: copy.start())
+            weights(cyc, True)
 
         if first < n_cyc:
             before = first - GROUP
@@ -179,7 +183,7 @@
                     halo_copy(slot, cyc).wait_send()
 
             for cyc in range(first + GROUP, first + 2 * GROUP):
-                weights(cyc, lambda copy: copy.wait())
+                weights(cyc, False)
 
             @pl.when(part == TEAM - 1)
             def _():
@@ -220,7 +224,7 @@
             skip_acc[seq, rows, :] += dot(acts[tile], w_sk[cyc])
 
     def out_copies(seq, step, remote):
-        place = (2 * ((me // 2 + step) % (per_part // 2)) + step // (per_part // 2)) % per_part
+        place = (2 * ((me // 2 + step * 3) % (per_part // 2)) + step // (per_part // 2)) % per_part
         target = part * per_part + place
         rows = pl.ds(place * block_len, block_len)
         which = team * TEAM + seq
@@ -276,7 +280,7 @@
         return 0
 
     for cyc in range(GROUP):
-        for copy in weight_copies(0, cyc):
+        for copy in weight_waits(cyc):
             copy.wait()
     lax.fori_loop(0, TEAM, one_sequence, 0)
 
@@ -334,7 +338,7 @@
                 pltpu.VMEM((TEAM * n_rep + 1, halo_rows, chans), jnp.bfloat16),
                 pltpu.VMEM((n_cyc, 5, chans, chans), jnp.bfloat16),
                 pltpu.VMEM((n_cyc, chans, skip_ch), jnp.bfloat16),
-                sem((n_cyc, 6)),
+                sem((n_cyc, 2)),
                 sem((TEAM, per_part)),
                 sem((TEAM, per_part)),
                 sem((n_cyc,)),

time: 146 us -> 144 us (0.986)
  the two profiles are of different devices: /device:TPU:105 before, /device:TPU:99 now
where the time goes in v3:
time: 144 us
  Pallas kernels  141 us (98%)
  local copies, waits for them, and re-layouts  2.29 us (2%)
    pallas_call x1, Pallas kernels, local_stack(): pl.pallas_call(functools.partial(stack_kernel, n_hi, n_lo, n_rep, n_cyc),...  141 us

profile of v3, /device:TPU:99, one launch (start us, length us, event | category | flops | bytes accessed | tf_op | source)
XLA Modules:
  0.0 144.0 jit_solution(6371726156518467324)
XLA Ops:
  0.6 141.1 %shard_map.86 = (f32[32,32,512]{2,1,0:T(8,128)S(1)}, f32[32,32,256]{2,1,0:T(8,128)S(1)}) custom-call(bf16[32,32,512]{2,1,0:T(8,128)(2,1)} %x_ref.1, bf16[3,10,512,512]{3,2,1,0:T(8,128)(2,1)} %wf0_ref.1, bf16[3,10,512,512]{3,2,1,0:T(8,128)(2,1)} %wf1_ref.1, bf16[3,10,512,512]{3,2,1,0:T(8,128)(2,1)} %wg0_ref.1, bf16[3,10,512,512]{3,2,1,0:T(8,128)(2,1)} %wg1_ref.1, ...), custom_call_target="tpu_custom_call" | custom-call | tf_op jit(solution)/shard_map/pallas_call | solution.py:328
  141.7 1.3 copy.11
  143.1 1.0 copy.12
